TPU v7x, 32 devices: a whole 2x2x4 slice. The times are simulated.
32 devices in a mesh: dp: 8 (over z, x), blk: 4 (over y, core).
Axes of the slice: x: 2, y: 2, z: 4, core: 2. Of those that a mesh axis runs over, the one named last changes fastest.
Arguments:
- queries: bfloat16 [8, 512, 2048], P('dp', 'blk'), may hold values from -6 to 6
- keys: bfloat16 [8, 512, 512], P('dp', 'blk'), may hold values from -6 to 6
- values: bfloat16 [8, 512, 512], P('dp', 'blk'), may hold values from -6 to 6
- out_grad: bfloat16 [8, 512, 2048], P('dp', 'blk'), may hold values from -6 to 6
- layer_input: bfloat16 [8, 512, 4096], P('dp', 'blk'), may hold values from -6 to 6
- lengths: int32 [8, 3], P('dp'), may hold values from 32 to 448, as said below
Outputs:
- query_grad: bfloat16 [8, 512, 2048], P('dp', 'blk')
- key_grad: bfloat16 [8, 512, 512], P('dp', 'blk')
- value_grad: bfloat16 [8, 512, 512], P('dp', 'blk')
- weight_grad: float32 [4096, 1024], P(('dp', 'blk'))
Inputs may be any that keep to these rules, and one draw needn't show every extreme that they name: `lengths`: each row sums to 512; the chosen and rejected counts lie between 32 and 96.
All inputs are finite; a program needn't handle non-finite values.
Results may differ from a plain program's by a relative error of at most 0.023.
Values may be sent and summed in bfloat16 or wider, within the bound.
A program may use at most 128 MiB of HBM per device.

v0:
```python
import math
import jax
import jax.numpy as jnp
from jax import lax
from jax.sharding import PartitionSpec as P

HEAD = 128
rope_base = 500000.0
masked_fill = -1e30


def stored_positions(stored_rows, shard_rows, shard_count):
    half_rows = shard_rows // 2
    block_number = stored_rows // half_rows
    holder = block_number // 2
    upper_half = block_number % 2
    position_block = jnp.where(upper_half == 1, 2 * shard_count - 1 - holder, holder)
    return (position_block * half_rows + stored_rows % half_rows).astype(jnp.int32)


def allowed_pairs(query_pos, key_pos, prompt_len, chosen_len):
    causal = key_pos[None, :] <= query_pos[:, None]
    reject_start = prompt_len + chosen_len
    query_rejected = query_pos >= reject_start
    key_chosen = jnp.logical_and(key_pos >= prompt_len, key_pos < reject_start)
    return jnp.logical_and(
        causal, jnp.logical_not(jnp.logical_and(query_rejected[:, None], key_chosen[None, :]))
    )


def block_length(total_rows):
    chosen_size = 1
    for candidate in range(1, min(total_rows, 512) + 1):
        if total_rows % candidate == 0:
            chosen_size = candidate
    return chosen_size


def over_blocks(running, pieces, first_row, block_fn):
    total_rows = pieces[0].shape[0]
    block_rows = block_length(total_rows)

    def one_turn(turn_index, current):
        block_start = turn_index * block_rows
        block_parts = tuple(
            (lax.dynamic_slice_in_dim(member, block_start, block_rows, 0) for member in pieces)
        )
        return block_fn(current, block_parts, first_row + block_start)

    return lax.fori_loop(0, total_rows // block_rows, one_turn, running)


def body(queries, keys, values, out_grad, layer_input, lengths):
    shard_count = lax.axis_size("blk")
    shard_index = lax.axis_index("blk")
    shard_rows = queries.shape[1]
    kv_heads = keys.shape[2] // HEAD
    group_heads = queries.shape[2] // keys.shape[2]
    seq_len = shard_rows * shard_count
    query_count = group_heads * shard_rows
    scale = 1.0 / math.sqrt(HEAD)
    prompt_len = lengths[0, 0]
    chosen_len = lengths[0, 1]
    own_rows = shard_index * shard_rows + jnp.arange(shard_rows, dtype=jnp.int32)
    own_pos = stored_positions(own_rows, shard_rows, shard_count)
    query_pos = jnp.tile(own_pos, group_heads)
    query_rows = (
        queries[0]
        .reshape(shard_rows, kv_heads, group_heads, HEAD)
        .transpose(1, 2, 0, 3)
        .reshape(kv_heads, query_count, HEAD)
    )
    grad_rows = (
        out_grad[0]
        .reshape(shard_rows, kv_heads, group_heads, HEAD)
        .transpose(1, 2, 0, 3)
        .reshape(kv_heads, query_count, HEAD)
    )

    def block_allowed(first_row, count_rows):
        key_pos = stored_positions(
            first_row + jnp.arange(count_rows, dtype=jnp.int32), shard_rows, shard_count
        )
        return allowed_pairs(query_pos, key_pos, prompt_len, chosen_len)

    def forward_block(running, block_parts, first_row):
        key_block, value_block = block_parts
        count_rows = key_block.shape[0]
        allowed = block_allowed(first_row, count_rows)
        run_max, run_sum, run_acc = running
        key_heads = key_block.reshape(count_rows, kv_heads, HEAD)
        value_heads = value_block.reshape(count_rows, kv_heads, HEAD).astype(jnp.float32)
        scores = scale * jnp.einsum(
            "gqe,kge->gqk", query_rows, key_heads, preferred_element_type=jnp.float32
        )
        new_max = jnp.maximum(
            run_max, jnp.max(jnp.where(allowed[None], scores, masked_fill), axis=-1)
        )
        weights = jnp.where(allowed[None], jnp.exp(scores - new_max[..., None]), 0.0)
        factor = jnp.exp(run_max - new_max)
        new_sum = run_sum * factor + jnp.sum(weights, axis=-1)
        new_acc = run_acc * factor[..., None] + jnp.einsum(
            "gqk,kge->gqe", weights, value_heads, precision=lax.Precision.HIGHEST
        )
        return (new_max, new_sum, new_acc)

    start_forward = (
        jnp.full((kv_heads, query_count), masked_fill, jnp.float32),
        jnp.zeros((kv_heads, query_count), jnp.float32),
        jnp.zeros((kv_heads, query_count, HEAD), jnp.float32),
    )
    run_max, run_sum, run_acc = over_blocks(
        start_forward,
        (
            lax.all_gather(keys[0], "blk", axis=0, tiled=True),
            lax.all_gather(values[0], "blk", axis=0, tiled=True),
        ),
        jnp.int32(0),
        forward_block,
    )
    attn_out = run_acc / run_sum[..., None]
    log_total = run_max + jnp.log(run_sum)
    delta = jnp.sum(grad_rows.astype(jnp.float32) * attn_out, axis=-1)

    def backward_block(running, block_parts, first_row):
        key_block, value_block = block_parts
        count_rows = key_block.shape[0]
        allowed = block_allowed(first_row, count_rows)
        query_acc, key_acc, value_acc = running
        key_heads = key_block.reshape(count_rows, kv_heads, HEAD)
        value_heads = value_block.reshape(count_rows, kv_heads, HEAD)
        scores = scale * jnp.einsum(
            "gqe,kge->gqk", query_rows, key_heads, preferred_element_type=jnp.float32
        )
        probs = jnp.where(allowed[None], jnp.exp(scores - log_total[..., None]), 0.0)
        prob_half = probs.astype(jnp.bfloat16)
        prob_grad = jnp.einsum(
            "gqe,kge->gqk", grad_rows, value_heads, preferred_element_type=jnp.float32
        )
        score_grad = (scale * probs * (prob_grad - delta[..., None])).astype(jnp.bfloat16)
        query_acc = query_acc + jnp.einsum(
            "gqk,kge->gqe", score_grad, key_heads, preferred_element_type=jnp.float32
        )
        key_term = jnp.einsum(
            "gqk,gqe->kge", score_grad, query_rows, preferred_element_type=jnp.float32
        ).reshape(count_rows, kv_heads * HEAD)
        value_term = jnp.einsum(
            "gqk,gqe->kge", prob_half, grad_rows, preferred_element_type=jnp.float32
        ).reshape(count_rows, kv_heads * HEAD)
        key_acc = lax.dynamic_update_slice_in_dim(
            key_acc,
            lax.dynamic_slice_in_dim(key_acc, first_row, count_rows, 0) + key_term,
            first_row,
            0,
        )
        value_acc = lax.dynamic_update_slice_in_dim(
            value_acc,
            lax.dynamic_slice_in_dim(value_acc, first_row, count_rows, 0) + value_term,
            first_row,
            0,
        )
        return (query_acc, key_acc, value_acc)

    start_backward = (
        jnp.zeros((kv_heads, query_count, HEAD), jnp.float32),
        jnp.zeros((seq_len, kv_heads * HEAD), jnp.float32),
        jnp.zeros((seq_len, kv_heads * HEAD), jnp.float32),
    )
    query_acc, key_acc, value_acc = over_blocks(
        start_backward,
        (
            lax.all_gather(keys[0], "blk", axis=0, tiled=True),
            lax.all_gather(values[0], "blk", axis=0, tiled=True),
        ),
        jnp.int32(0),
        backward_block,
    )
    key_sum, value_sum = (
        lax.psum_scatter(
            key_acc.astype(jnp.bfloat16), "blk", scatter_dimension=0, tiled=True
        ).astype(jnp.float32),
        lax.psum_scatter(
            value_acc.astype(jnp.bfloat16), "blk", scatter_dimension=0, tiled=True
        ).astype(jnp.float32),
    )
    query_grad = (
        query_acc.reshape(kv_heads, group_heads, shard_rows, HEAD)
        .transpose(2, 0, 1, 3)
        .reshape(shard_rows, kv_heads * group_heads * HEAD)
        .astype(jnp.bfloat16)
    )
    key_out = key_sum.astype(jnp.bfloat16)
    value_out = value_sum.astype(jnp.bfloat16)
    half_dim = HEAD // 2
    frequency = jnp.exp(
        -(2.0 * jnp.arange(half_dim, dtype=jnp.float32) / HEAD) * math.log(rope_base)
    )
    angles = own_pos.astype(jnp.float32)[:, None] * frequency[None, :]
    cosine = jnp.concatenate([jnp.cos(angles), jnp.cos(angles)], axis=-1)[:, None, :]
    sine = jnp.concatenate([jnp.sin(angles), jnp.sin(angles)], axis=-1)[:, None, :]
    grad_heads = key_sum.reshape(shard_rows, kv_heads, HEAD)
    rotated = jnp.concatenate([-grad_heads[..., half_dim:], grad_heads[..., :half_dim]], axis=-1)
    key_pre = (
        (grad_heads * cosine - rotated * sine)
        .reshape(shard_rows, kv_heads * HEAD)
        .astype(jnp.bfloat16)
    )
    grad_cols = jnp.concatenate([key_pre, value_out], axis=1)
    input_rows = layer_input[0]
    features = layer_input.shape[2]
    replica_count = lax.axis_size("dp")
    feature_share = features // (replica_count * shard_count)
    grouped_input = input_rows.reshape(shard_rows, replica_count, shard_count * feature_share)
    sequence_input = lax.all_to_all(grouped_input, "blk", split_axis=2, concat_axis=0, tiled=True)
    sequence_weight = jnp.einsum(
        "tif,tc->ifc",
        sequence_input,
        lax.all_gather(grad_cols, "blk", axis=0, tiled=True),
        preferred_element_type=jnp.float32,
    )
    weight_grad = (
        lax.psum_scatter(
            sequence_weight.astype(jnp.bfloat16), "dp", scatter_dimension=0, tiled=True
        )
        .astype(jnp.float32)
        .reshape(feature_share, grad_cols.shape[1])
    )
    return (query_grad[None], key_out[None], value_out[None], weight_grad)


def solution(mesh):
    placed = (
        P("dp", "blk", None),
        P("dp", "blk", None),
        P("dp", "blk", None),
        P("dp", "blk", None),
        P("dp", "blk", None),
        P("dp", None),
    )
    return jax.shard_map(
        body,
        mesh=mesh,
        in_specs=placed,
        out_specs=(
            P("dp", "blk", None),
            P("dp", "blk", None),
            P("dp", "blk", None),
            P(("dp", "blk"), None),
        ),
        check_vma=False,
    )
```

profile of v0, /device:TPU:0, one launch (start us, length us, event | category | flops | bytes accessed | tf_op | source)
XLA Modules:
  0.0 209.5 jit_solution(16172209524626766928)
XLA Ops:
  7.2 0.0 reduce-scatter.10.cloned.1.call-start
  7.2 1.3 fusion.41
  9.9 0.7 compare_and_fusion
  10.6 1.4 reshape_squeeze.9
  12.0 0.6 copy.85
  12.6 0.2 reshape.331
  12.8 1.0 copy.86
  13.8 8.7 %all-gather = bf16[1,512,512]{1,2,0:T(8,128)(2,1)S(1)} all-gather(bf16[1,128,512]{1,2,0:T(8,128)(2,1)S(1)} %copy.86), channel_id=2, replica_groups=mesh['dp'=8,'blk'=4] {'blk'}, dimensions={1}, use_global_device_ids=true | all-gather | bytes 655360 | tf_op jit(solution)/shard_map/all_gather | solution.py:172
  22.5 0.3 not_and_fusion
  22.8 0.0 copy-start.2
  22.8 1.0 select_reduce_fusion
  23.8 0.0 copy-start
  23.8 0.0 copy-start.4
  23.8 1.9 copy-done
  25.7 0.9 fusion.1
  26.6 0.0 copy-done.2
  26.6 0.4 reshape_squeeze.10
  27.0 0.6 copy.89
  27.6 0.2 reshape.333
  27.8 0.0 copy-done.4
  27.8 0.0 copy-start.3
  27.8 0.1 copy.90
  28.0 7.3 %all-gather.1 = bf16[1,512,512]{1,2,0:T(8,128)(2,1)S(1)} all-gather(bf16[1,128,512]{1,2,0:T(8,128)(2,1)S(1)} %copy.90), channel_id=3, replica_groups=mesh['dp'=8,'blk'=4] {'blk'}, dimensions={1}, use_global_device_ids=true | all-gather | bytes 655360 | tf_op jit(solution)/shard_map/all_gather | solution.py:173
  35.3 0.0 copy-start.1
  35.3 4.9 %multiply_reduce_fusion = f32[4,512]{1,0:T(4,128)S(1)} fusion(bf16[4,512,128]{1,2,0:T(8,128)(2,1)S(1)} %reshape.333, bf16[512,4,128]{0,2,1:T(8,128)(2,1)S(1)} %bitcast.73, f32[4,512,512]{1,2,0:T(8,128)} %copy-done, f32[4,512]{1,0:T(4,128)S(1)} %broadcast_maximum_fusion, pred[512,512]{0,1:T(8,128)(4,1)S(1)} %not_and_fusion, ...), kind=kOutput, calls=%fused_computation.22 | convolution fusion | flops 1615067136 | bytes 5537792 | tf_op jit(solution)/shard_map/while/body/eval_jaxpr/gqk,kge->gqe/dot_general | solution.py:102
  40.2 0.0 copy-done.3
  40.2 0.0 copy-done.1
  40.2 2.7 %multiply_convert_fusion = bf16[4,512,512]{1,2,0:T(8,128)(2,1)S(1)} fusion(f32[4,512,512]{1,2,0:T(8,128)S(1)} %copy-done.1, bf16[4,512,128]{1,2,0:T(8,128)(2,1)} %copy-done.3, bf16[512,4,128]{0,2,1:T(8,128)(2,1)S(1)} %bitcast.74, f32[4,512]{1,0:T(4,128)S(1)} %multiply_reduce_fusion, f32[4,512]{1,0:T(4,128)S(1)} %get-tuple-element.90, ...), kind=kOutput, calls=%fused_computation | convolution fusion | flops 275775488 | bytes 7618560 | tf_op jit(solution)/shard_map/while/body/eval_jaxpr/gqe,kge->gqk/dot_general | solution.py:137
  42.9 1.6 convolution_convert_fusion
  44.5 2.1 copy.117
  46.6 0.0 reduce-scatter.10.cloned.1.call-update
  46.6 0.0 reduce-scatter.12.cloned.1.call-start
  46.6 3.4 %fusion.14 = bf16[4,512,128]{1,2,0:T(8,128)(2,1)S(1)} fusion(bf16[4,512,128]{1,2,0:T(8,128)(2,1)} %copy-done.3, f32[4,512,512]{1,2,0:T(8,128)} %copy-done, f32[4,512]{1,0:T(4,128)S(1)} %get-tuple-element.90, pred[512,512]{0,1:T(8,128)(4,1)S(1)} %not_and_fusion), kind=kOutput, calls=%fused_computation.20 | convolution fusion | flops 272891904 | bytes 5513216 | tf_op jit(solution)/shard_map/while/body/eval_jaxpr/gqk,gqe->kge/dot_general | solution.py:147
  50.0 1.0 copy.119
  51.0 0.0 reduce-scatter.12.cloned.1.call-update
  51.0 0.0 all-gather.4.cloned.1.call-start
  51.1 0.2 multiply_cosine_fusion
  51.3 18.0 %reduce-scatter.10.cloned.1.call-done = bf16[128,512]{1,0:T(8,128)(2,1)} async-done(((bf16[512,512]{1,0:T(8,128)(2,1)}), bf16[128,512]{1,0:T(8,128)(2,1)}) %reduce-scatter.10.cloned.1.call-update) | async-done | bytes 131088
  69.3 1.0 copy.118
  70.5 23.6 %reduce-scatter.12.cloned.1.call-done = bf16[128,512]{1,0:T(8,128)(2,1)} async-done(((bf16[512,512]{1,0:T(8,128)(2,1)}), bf16[128,512]{1,0:T(8,128)(2,1)}) %reduce-scatter.12.cloned.1.call-update) | async-done | bytes 131088
  94.0 1.0 copy.120
  95.1 0.7 pad_maximum_fusion
  95.8 0.0 all-gather.4.cloned.1.call-update
  95.8 0.2 reduce-scatter.8.cloned.1.call-start
  96.0 2.3 %copy.100 = bf16[1,128,4096]{1,2,0:T(8,128)(2,1)} copy(bf16[1,128,4096]{2,1,0:T(8,128)(2,1)} %param.10) | data formatting | bytes 2097152 | tf_op args[4]
  98.3 1.9 copy.101
  100.2 22.5 %all_to_all.18 = bf16[128,8,512]{0,1,2:T(8,128)(2,1)} all-to-all(bf16[128,8,512]{0,1,2:T(8,128)(2,1)S(1)} %copy.101), channel_id=1, replica_groups=mesh['dp'=8,'blk'=4] {'blk'}, dimensions={2} | all-to-all | bytes 2097152 | tf_op jit(solution)/shard_map/all_to_all | solution.py:214
  122.8 3.0 %copy.102 = bf16[128,8,512]{2,1,0:T(8,128)(2,1)} copy(bf16[128,8,512]{0,1,2:T(8,128)(2,1)} %all_to_all.18) | data formatting | bytes 2097152 | tf_op jit(solution)/shard_map/all_to_all | solution.py:214
  125.8 2.6 %copy.103 = bf16[4,128,8,128]{3,1,0,2:T(8,128)(2,1)} copy(bf16[4,128,8,128]{3,2,0,1:T(8,128)(2,1)} %bitcast.62) | data formatting | bytes 2097152 | tf_op jit(solution)/shard_map/all_to_all | solution.py:214
  128.4 0.0 all-gather.4.cloned.1.call-done
  128.4 4.1 %convert_bitcast_fusion = bf16[8,128,1024]{1,2,0:T(8,128)(2,1)} fusion(bf16[512,8,128]{2,0,1:T(8,128)(2,1)} %bitcast.72, bf16[512,1024]{0,1:T(8,128)(2,1)} %all-gather.4.cloned.1.call-done), kind=kOutput, calls=%fused_computation.8 | convolution fusion | flops 1074790400 | bytes 4194304 | tf_op jit(solution)/shard_map/tif,tc->ifc/dot_general | solution.py:215
  132.5 0.0 reduce-scatter.8.cloned.1.call-update
  132.5 0.9 convolution_convert_fusion.1
  133.4 0.4 copy.97
  133.8 1.2 convert_element_type.78
  135.0 0.8 copy.105
  135.8 0.8 copy.104
  136.6 64.5 %reduce-scatter.8.cloned.1.call-done = bf16[1,128,1024]{1,2,0:T(8,128)(2,1)} async-done(((bf16[8,128,1024]{1,2,0:T(8,128)(2,1)}), bf16[1,128,1024]{1,2,0:T(8,128)(2,1)}) %reduce-scatter.8.cloned.1.call-update) | async-done | bytes 262160 | tf_op jit(solution)/shard_map/reduce_scatter | solution.py:222
  201.0 1.0 bitcast_convert_fusion
  202.0 1.0 copy.106
  (14 shorter events, 0.2 us)
Async XLA Ops:
  7.2 62.1 %reduce-scatter.10.cloned.1.call-start = ((), (), s32[]{:S(2)}) async-start(), calls=%async_computation.6 | async-start | bytes 655360
  22.8 3.9 %copy-start.2 = (bf16[1,128,2048]{2,1,0:T(8,128)(2,1)S(1)}, bf16[1,128,2048]{2,1,0:T(8,128)(2,1)}, u32[]{:S(2)}) copy-start(bf16[1,128,2048]{2,1,0:T(8,128)(2,1)} %param.9) | copy-start | bytes 1572868
  23.8 1.9 copy-start
  23.8 4.0 %copy-start.4 = (bf16[1,128,512]{2,1,0:T(8,128)(2,1)S(1)}, bf16[1,128,512]{2,1,0:T(8,128)(2,1)}, u32[]{:S(2)}) copy-start(bf16[1,128,512]{2,1,0:T(8,128)(2,1)} %param.8) | copy-start | bytes 393220
  27.8 12.4 %copy-start.3 = (bf16[4,512,128]{1,2,0:T(8,128)(2,1)}, bf16[4,512,128]{1,2,0:T(8,128)(2,1)S(1)}, u32[]{:S(2)}) copy-start(bf16[4,512,128]{1,2,0:T(8,128)(2,1)S(1)} %reshape.333) | copy-start | bytes 1572868
  35.3 4.9 %copy-start.1 = (f32[4,512,512]{1,2,0:T(8,128)S(1)}, f32[4,512,512]{1,2,0:T(8,128)}, u32[]{:S(2)}) copy-start(f32[4,512,512]{1,2,0:T(8,128)} %copy-done) | copy-start | bytes 12582916
  46.6 47.5 %reduce-scatter.12.cloned.1.call-start = ((), (), s32[]{:S(2)}) async-start(), calls=%async_computation.7 | async-start | bytes 655360
  51.0 77.3 %all-gather.4.cloned.1.call-start = ((), (), s32[]{:S(2)}) async-start(), calls=%async_computation.4 | async-start | bytes 1310720 | tf_op jit(solution)/shard_map/all_gather | solution.py:218
  95.8 105.2 %reduce-scatter.8.cloned.1.call-start = ((), (), s32[]{:S(2)}) async-start(), calls=%async_computation.5 | async-start | bytes 2359296 | tf_op jit(solution)/shard_map/reduce_scatter | solution.py:222
Sparse Core Ops, SparseCore 0:
  46.7 22.5 reduce-scatter.9
  72.4 21.6 reduce-scatter.11
  96.2 22.0 all-gather.3
  132.6 68.3 reduce-scatter.7
where the time goes:
time: 210 us
  waiting for transfers between devices  106 us (50%)
  blocking collectives  38.5 us (18%)
  local copies, waits for them, and re-layouts  26.8 us (13%)
  matrix products  18.5 us (9%)
  between operations  15.3 us (7%)
  other arithmetic  3.97 us (2%)
    reduce_scatter x1, waiting for transfers between devices, body(): lax.psum_scatter(sequence_weight.astype(jnp.bfloat16), 'dp', scatter_dime...  64.5 us
    unnamed x6, waiting for transfers between devices  41.6 us
    all_to_all x1, blocking collectives, body(): lax.all_to_all(grouped_input, 'blk', split_axis=2, concat_axis=0, tiled=T...  22.5 us
    unnamed x20, local copies, waits for them, and re-layouts  13 us
    all_gather x1, blocking collectives, body(): lax.all_gather(keys[0], 'blk', axis=0, tiled=True)  8.68 us
    all_gather x1, blocking collectives, body(): lax.all_gather(values[0], 'blk', axis=0, tiled=True)  7.29 us
    all_to_all x2, local copies, waits for them, and re-layouts, body(): lax.all_to_all(grouped_input, 'blk', split_axis=2, concat_axis=0, tiled=T...  5.62 us
    dot_general x1, matrix products, forward_block(): jnp.einsum('gqk,kge->gqe', weights, value_heads, precision=lax.Precision....  4.93 us
  transfers between devices with their start and end apart: 4, of which 3 were waited for; matrix products, arithmetic and copies ran while one was open for 9% of the time, Pallas kernels for 0%

commit v1 on v0

--- a/solution.py
+++ b/solution.py
@@ -211,7 +211,12 @@
     replica_count = lax.axis_size("dp")
     feature_share = features // (replica_count * shard_count)
     grouped_input = input_rows.reshape(shard_rows, replica_count, shard_count * feature_share)
-    sequence_input = lax.all_to_all(grouped_input, "blk", split_axis=2, concat_axis=0, tiled=True)
+    sequence_input = jnp.concatenate(
+        lax.all_to_all(
+            jnp.stack(jnp.split(grouped_input, lax.axis_size("blk"), axis=2)), "blk", 0, 0
+        ),
+        axis=0,
+    )
     sequence_weight = jnp.einsum(
         "tif,tc->ifc",
         sequence_input,

time: 210 us -> 203 us (0.967)
  local copies, waits for them, and re-layouts: 26.8 us -> 15.2 us
  other arithmetic: 3.97 us -> 7.34 us
    unnamed x6 -> x4, waiting for transfers between devices: 41.6 us -> 0.07 us
    reduce_scatter x0 -> x2, waiting for transfers between devices: none -> 40 us  [the longest x1 22.3 us: body(): lax.psum_scatter(value_acc.astype(jnp.bfloat16), 'blk', scatter_dimension...]
    unnamed x20 -> x13, local copies, waits for them, and re-layouts: 13 us -> 4.7 us
    all_to_all x2 -> x0, local copies, waits for them, and re-layouts: 5.62 us -> none  [body(): lax.all_to_all(grouped_input, 'blk', split_axis=2, concat_axis=0, tiled=T...]
    convert_element_type x0 -> x2, local copies, waits for them, and re-layouts: none -> 3.06 us  [the longest x1 2.05 us: body(): key_acc.astype(jnp.bfloat16)]
  transfers between devices with their start and end apart: 4 -> 4, of which waited for: 3 -> 3; matrix products, arithmetic and copies ran while one was open for 9% -> 6% of each run, Pallas kernels for 0% -> 0%
where the time goes in v1:
time: 203 us; the launch traced here: 202 us
  waiting for transfers between devices  106 us (52%)
  blocking collectives  39.2 us (19%)
  matrix products  18.6 us (9%)
  between operations  15.3 us (8%)
  local copies, waits for them, and re-layouts  15.2 us (7%)
  other arithmetic  7.34 us (4%)
    reduce_scatter x1, waiting for transfers between devices, body(): lax.psum_scatter(sequence_weight.astype(jnp.bfloat16), 'dp', scatter_dime...  66.1 us
    all_to_all x1, blocking collectives, body(): lax.all_to_all(jnp.stack(jnp.split(grouped_input, lax.axis_size('blk'), a...  23.2 us
    reduce_scatter x1, waiting for transfers between devices, body(): lax.psum_scatter(value_acc.astype(jnp.bfloat16), 'blk', scatter_dimension...  22.3 us
    reduce_scatter x1, waiting for transfers between devices, body(): lax.psum_scatter(key_acc.astype(jnp.bfloat16), 'blk', scatter_dimension=0...  17.7 us
    all_gather x1, blocking collectives, body(): lax.all_gather(keys[0], 'blk', axis=0, tiled=True)  8.68 us
    all_gather x1, blocking collectives, body(): lax.all_gather(values[0], 'blk', axis=0, tiled=True)  7.29 us
    dot_general x1, matrix products, forward_block(): jnp.einsum('gqk,kge->gqe', weights, value_heads, precision=lax.Precision....  4.93 us
    unnamed x13, local copies, waits for them, and re-layouts  4.7 us
  transfers between devices with their start and end apart: 4, of which 3 were waited for; matrix products, arithmetic and copies ran while one was open for 6% of the time, Pallas kernels for 0%

profile of v1, /device:TPU:0, one launch (start us, length us, event | category | flops | bytes accessed | tf_op | source)
XLA Modules:
  0.0 202.2 jit_solution(17738924869191291380)
XLA Ops:
  7.2 0.0 reduce-scatter.4.cloned.1.call-start
  7.2 1.3 fusion.42
  9.9 0.7 compare_and_fusion
  10.6 1.4 reshape_squeeze.9
  12.0 0.6 copy.27
  12.6 0.2 reshape.334
  12.8 1.0 copy.28
  13.8 8.7 %all-gather = bf16[1,512,512]{1,2,0:T(8,128)(2,1)S(1)} all-gather(bf16[1,128,512]{1,2,0:T(8,128)(2,1)S(1)} %copy.28), channel_id=2, replica_groups=mesh['dp'=8,'blk'=4] {'blk'}, dimensions={1}, use_global_device_ids=true | all-gather | bytes 655360 | tf_op jit(solution)/shard_map/all_gather | solution.py:172
  22.5 0.3 not_and_fusion
  22.8 0.0 copy-start.2
  22.8 1.0 select_reduce_fusion
  23.8 0.0 copy-start
  23.8 0.0 copy-start.4
  23.8 1.9 copy-done
  25.7 0.9 fusion.1
  26.6 0.0 copy-done.2
  26.7 0.4 reshape_squeeze.10
  27.0 0.6 copy.31
  27.6 0.2 reshape.336
  27.8 0.0 copy-done.4
  27.8 0.0 copy-start.3
  27.8 0.1 copy.32
  28.0 7.3 %all-gather.1 = bf16[1,512,512]{1,2,0:T(8,128)(2,1)S(1)} all-gather(bf16[1,128,512]{1,2,0:T(8,128)(2,1)S(1)} %copy.32), channel_id=3, replica_groups=mesh['dp'=8,'blk'=4] {'blk'}, dimensions={1}, use_global_device_ids=true | all-gather | bytes 655360 | tf_op jit(solution)/shard_map/all_gather | solution.py:173
  35.3 0.0 copy-start.1
  35.3 4.9 %multiply_reduce_fusion = f32[4,512]{1,0:T(4,128)S(1)} fusion(bf16[4,512,128]{1,2,0:T(8,128)(2,1)S(1)} %reshape.336, bf16[512,4,128]{0,2,1:T(8,128)(2,1)S(1)} %bitcast.73, f32[4,512,512]{1,2,0:T(8,128)} %copy-done, f32[4,512]{1,0:T(4,128)S(1)} %broadcast_maximum_fusion, pred[512,512]{0,1:T(8,128)(4,1)S(1)} %not_and_fusion, ...), kind=kOutput, calls=%fused_computation.24 | convolution fusion | flops 1615067136 | bytes 5537792 | tf_op jit(solution)/shard_map/while/body/eval_jaxpr/gqk,kge->gqe/dot_general | solution.py:102
  40.2 0.0 copy-done.3
  40.2 0.0 copy-done.1
  40.2 2.7 %multiply_convert_fusion = bf16[4,512,512]{1,2,0:T(8,128)(2,1)S(1)} fusion(f32[4,512,512]{1,2,0:T(8,128)S(1)} %copy-done.1, bf16[4,512,128]{1,2,0:T(8,128)(2,1)} %copy-done.3, bf16[512,4,128]{0,2,1:T(8,128)(2,1)S(1)} %bitcast.74, f32[4,512]{1,0:T(4,128)S(1)} %multiply_reduce_fusion, f32[4,512]{1,0:T(4,128)S(1)} %get-tuple-element.61, ...), kind=kOutput, calls=%fused_computation | convolution fusion | flops 275775488 | bytes 7618560 | tf_op jit(solution)/shard_map/while/body/eval_jaxpr/gqe,kge->gqk/dot_general | solution.py:137
  42.9 1.6 convolution_convert_fusion.1
  44.5 2.1 %copy.41 = bf16[512,512]{1,0:T(8,128)(2,1)} copy(bf16[512,512]{0,1:T(8,128)(2,1)} %bitcast.69) | data formatting | bytes 1048576 | tf_op jit(solution)/shard_map/convert_element_type | solution.py:180
  46.6 0.0 reduce-scatter.4.cloned.1.call-update
  46.6 0.0 reduce-scatter.6.cloned.1.call-start
  46.6 3.4 %fusion.14 = bf16[4,512,128]{1,2,0:T(8,128)(2,1)S(1)} fusion(bf16[4,512,128]{1,2,0:T(8,128)(2,1)} %copy-done.3, f32[4,512,512]{1,2,0:T(8,128)} %copy-done, f32[4,512]{1,0:T(4,128)S(1)} %get-tuple-element.61, pred[512,512]{0,1:T(8,128)(4,1)S(1)} %not_and_fusion), kind=kOutput, calls=%fused_computation.20 | convolution fusion | flops 272891904 | bytes 5513216 | tf_op jit(solution)/shard_map/while/body/eval_jaxpr/gqk,gqe->kge/dot_general | solution.py:147
  50.0 1.0 copy.43
  51.0 0.0 reduce-scatter.6.cloned.1.call-update
  51.0 0.0 all-gather.4.cloned.1.call-start
  51.1 0.3 multiply_cosine_fusion
  51.4 0.1 pad_maximum_fusion.3
  51.5 0.1 pad_maximum_fusion.2
  51.6 17.7 %reduce-scatter.4.cloned.1.call-done = bf16[128,512]{1,0:T(8,128)(2,1)} async-done(((bf16[512,512]{1,0:T(8,128)(2,1)}), bf16[128,512]{1,0:T(8,128)(2,1)}) %reduce-scatter.4.cloned.1.call-update) | async-done | bytes 131088 | tf_op jit(solution)/shard_map/reduce_scatter | solution.py:179
  69.3 1.0 reshape.339
  70.3 0.2 slice_negate_fusion
  70.5 0.2 maximum_multiply_fusion
  70.8 1.0 fusion.19
  71.7 22.3 %reduce-scatter.6.cloned.1.call-done = bf16[128,512]{1,0:T(8,128)(2,1)} async-done(((bf16[512,512]{1,0:T(8,128)(2,1)}), bf16[128,512]{1,0:T(8,128)(2,1)}) %reduce-scatter.6.cloned.1.call-update) | async-done | bytes 131088 | tf_op jit(solution)/shard_map/reduce_scatter | solution.py:182
  94.1 1.6 pad_maximum_fusion.1
  95.7 0.0 all-gather.4.cloned.1.call-update
  95.7 0.2 reduce-scatter.8.cloned.1.call-start
  95.9 1.6 copy.56
  97.6 0.2 slice_bitcast_fusion.3
  97.8 0.1 pad_maximum_fusion
  97.9 23.2 %all_to_all.5 = bf16[4,128,8,128]{3,2,1,0:T(8,128)(2,1)} all-to-all(bf16[4,128,8,128]{3,2,1,0:T(8,128)(2,1)S(1)} %pad_maximum_fusion), channel_id=1, replica_groups=mesh['dp'=8,'blk'=4] {'blk'}, dimensions={0} | all-to-all | bytes 2097152 | tf_op jit(solution)/shard_map/all_to_all | solution.py:215
  121.1 0.0 all-gather.4.cloned.1.call-done
  121.1 4.2 %convolution_convert_fusion = bf16[8,128,1024]{2,1,0:T(8,128)(2,1)} fusion(bf16[512,1024]{1,0:T(8,128)(2,1)} %all-gather.4.cloned.1.call-done, bf16[512,8,128]{2,1,0:T(8,128)(2,1)} %bitcast.65), kind=kOutput, calls=%fused_computation.16 | convolution fusion | flops 1074790400 | bytes 4194304 | tf_op jit(solution)/shard_map/tif,tc->ifc/dot_general | solution.py:220
  125.3 0.0 reduce-scatter.8.cloned.1.call-update
  125.3 0.9 convolution_convert_fusion.2
  126.2 0.4 copy.39
  126.6 1.2 convert_element_type.75
  127.8 66.1 %reduce-scatter.8.cloned.1.call-done = bf16[1,128,1024]{2,1,0:T(8,128)(2,1)} async-done(((bf16[8,128,1024]{2,1,0:T(8,128)(2,1)}), bf16[1,128,1024]{2,1,0:T(8,128)(2,1)}) %reduce-scatter.8.cloned.1.call-update) | async-done | bytes 262160 | tf_op jit(solution)/shard_map/reduce_scatter | solution.py:227
  193.9 1.8 bitcast_convert_fusion
  (8 shorter events, 0.1 us)
Async XLA Ops:
  7.2 62.1 %reduce-scatter.4.cloned.1.call-start = ((), (), s32[]{:S(2)}) async-start(), calls=%async_computation.4 | async-start | bytes 655360 | tf_op jit(solution)/shard_map/reduce_scatter | solution.py:179
  22.8 3.9 %copy-start.2 = (bf16[1,128,2048]{2,1,0:T(8,128)(2,1)S(1)}, bf16[1,128,2048]{2,1,0:T(8,128)(2,1)}, u32[]{:S(2)}) copy-start(bf16[1,128,2048]{2,1,0:T(8,128)(2,1)} %param.9) | copy-start | bytes 1572868
  23.8 1.9 copy-start
  23.8 4.1 %copy-start.4 = (bf16[1,128,512]{2,1,0:T(8,128)(2,1)S(1)}, bf16[1,128,512]{2,1,0:T(8,128)(2,1)}, u32[]{:S(2)}) copy-start(bf16[1,128,512]{2,1,0:T(8,128)(2,1)} %param.8) | copy-start | bytes 393220
  27.8 12.4 %copy-start.3 = (bf16[4,512,128]{1,2,0:T(8,128)(2,1)}, bf16[4,512,128]{1,2,0:T(8,128)(2,1)S(1)}, u32[]{:S(2)}) copy-start(bf16[4,512,128]{1,2,0:T(8,128)(2,1)S(1)} %reshape.336) | copy-start | bytes 1572868
  35.3 4.9 %copy-start.1 = (f32[4,512,512]{1,2,0:T(8,128)S(1)}, f32[4,512,512]{1,2,0:T(8,128)}, u32[]{:S(2)}) copy-start(f32[4,512,512]{1,2,0:T(8,128)} %copy-done) | copy-start | bytes 12582916
  46.6 47.5 %reduce-scatter.6.cloned.1.call-start = ((), (), s32[]{:S(2)}) async-start(), calls=%async_computation.5 | async-start | bytes 655360 | tf_op jit(solution)/shard_map/reduce_scatter | solution.py:182
  51.0 70.1 %all-gather.4.cloned.1.call-start = ((), (), s32[]{:S(2)}) async-start(), calls=%async_computation.6 | async-start | bytes 1310720 | tf_op jit(solution)/shard_map/all_gather | solution.py:223
  95.7 98.2 %reduce-scatter.8.cloned.1.call-start = ((), (), s32[]{:S(2)}) async-start(), calls=%async_computation.7 | async-start | bytes 2359296 | tf_op jit(solution)/shard_map/reduce_scatter | solution.py:227
Sparse Core Ops, SparseCore 0:
  46.7 22.5 reduce-scatter.3
  72.3 21.6 reduce-scatter.5
  96.2 22.4 all-gather.3
  125.4 68.4 reduce-scatter.7
